TPU v7x, 512 devices: a whole 4x4x16 slice. The times are simulated.
512 devices in a mesh: seq: 128 (over x, z, core), head: 4 (over y).
Axes of the slice: x: 4, y: 4, z: 16, core: 2. Of those that a mesh axis runs over, the one named last changes fastest.
Arguments:
- values_in: bfloat16 [65536, 4096], P('seq', 'head'), may hold values from -6 to 6
- gate_in: bfloat16 [65536, 4096], P('seq', 'head'), may hold values from -6 to 6
- key_proj: bfloat16 [65536, 128], P('seq'), may hold values from -0.52734375 to 0.52734375
- query_proj: bfloat16 [65536, 128], P('seq'), may hold values from -6 to 6
- step_size: float32 [65536, 64], P('seq', 'head'), may hold values from 0.5 to 2
- log_decay: float32 [65536, 64], P('seq', 'head'), may hold values from -1.2 to 0
- skip_weight: float32 [64], P('head'), may hold values from 0.5 to 1.5
- norm_gain: float32 [4096], P('head'), may hold values from 0.5 to 1.5
- level_table: float32 [16, 64, 11], P(None, 'head'), may hold values from 0.25 to 2
- level_pick: int32 [65536], P('seq'), may hold values from 0 to 15
- doc_start: int32 [1024], P('seq'), may hold values 0 or 1
Outputs:
- layer_out: bfloat16 [65536, 4096], P('seq', 'head')
All inputs are finite; a program needn't handle non-finite values. No bound on the sum of `doc_start` on one device may be relied on, other than what follows from the above.
Results may differ from a plain program's by a relative error of at most 0.012.
Values may be sent and summed in bfloat16 or wider, within the bound.
A program may use at most 64 MiB of HBM per device.

v0:
```python
import math
import jax
import jax.numpy as jnp
from jax import lax
from jax.sharding import Mesh
from jax.sharding import PartitionSpec as P

H = 64
HEADDIM = 64
STRETCH = 64
SEQ = ("seq_0", "seq_1", "seq_2")
epsilon = 1e-06


def joined_along(pieces, dim):
    pieces = jnp.moveaxis(pieces, 0, dim)
    shape = pieces.shape
    return pieces.reshape(*shape[:dim], shape[dim] * shape[dim + 1], *shape[dim + 2 :])


def gather_in_order(array, axes, turns):
    pieces = array[None]
    for k in turns:
        pieces = lax.all_gather(pieces, axes[k], axis=0, tiled=True)
    current = [lax.axis_size(axes[k]) for k in reversed(turns)]
    pieces = pieces.reshape(*current, *array.shape)
    turned = sorted(range(len(turns)), key=lambda place: turns[len(turns) - 1 - place])
    return pieces.transpose(*turned, *range(len(turns), pieces.ndim)).reshape(-1, *array.shape)


def gathered_by_axis(array, axes, turns, dim):
    return joined_along(gather_in_order(array, axes, turns), dim)


def copy_for_each(array, axis):
    size = lax.axis_size(axis)
    return lax.all_to_all(
        jnp.broadcast_to(array[None], (size, *array.shape)), axis, 0, 0, tiled=True
    )


def over_copies(array, axis):
    everything = copy_for_each(array, axis)
    return jnp.sum(everything, axis=0)


def level_of_pairs(row_count, stretch_len, low_bits):
    blocks = jnp.arange(row_count, dtype=jnp.int32) // stretch_len
    differ = jnp.bitwise_xor(blocks[:, None], blocks[None, :])
    level_index = jnp.zeros((row_count, row_count), jnp.int32)
    for bit_index in range(low_bits):
        level_index = level_index + (differ >= 1 << bit_index).astype(jnp.int32)
    return level_index


def flip_pairs(tensor, bit_index):
    split_view = tensor.reshape(
        (tensor.shape[0] >> bit_index + 1, 2, 1 << bit_index) + tensor.shape[1:]
    )
    return split_view[:, ::-1].reshape(tensor.shape)


def local(
    values_in,
    gate_in,
    key_proj,
    query_proj,
    step_size,
    log_decay,
    skip_weight,
    norm_gain,
    level_table,
    level_pick,
    doc_start,
):
    tok_rows = values_in.shape[0]
    head_count = step_size.shape[1]
    head_width = HEADDIM
    state_width = key_proj.shape[1]
    per_span = doc_start.shape[0]
    low_bits = per_span.bit_length() - 1
    span_total = lax.axis_size(SEQ)
    span_bits = span_total.bit_length() - 1
    table_rows = level_table.shape[0]
    level_count = level_table.shape[2]
    one_hot = (level_pick[:, None] == jnp.arange(table_rows, dtype=jnp.int32)[None, :]).astype(
        jnp.float32
    )
    level_weight = jnp.dot(
        one_hot,
        level_table.reshape(table_rows, head_count * level_count),
        precision=lax.Precision.HIGHEST,
        preferred_element_type=jnp.float32,
    ).reshape(tok_rows, head_count, level_count)
    log_total = jnp.cumsum(log_decay, axis=0)
    doc_stretch = jnp.cumsum(doc_start)
    doc_count = jnp.broadcast_to(doc_stretch[:, None], (per_span, STRETCH)).reshape(tok_rows)
    scaled_in = (jnp.repeat(step_size, head_width, axis=1) * values_in.astype(jnp.float32)).astype(
        jnp.bfloat16
    )
    end_log = log_total[tok_rows - 1]
    tail_decay = (
        jnp.exp(end_log[None, :] - log_total)
        * (doc_count == doc_count[tok_rows - 1]).astype(jnp.float32)[:, None]
    )
    carried_in = (
        jnp.repeat(tail_decay, head_width, axis=1) * scaled_in.astype(jnp.float32)
    ).astype(jnp.bfloat16)
    end_state = jnp.einsum("sc,sn->cn", carried_in, key_proj, preferred_element_type=jnp.float32)
    span_decay = jnp.exp(end_log) * (doc_count[tok_rows - 1] == 0).astype(jnp.float32)
    own_index = lax.axis_index(SEQ)
    row_share = head_count * head_width // span_total
    pieces = lax.all_to_all(
        end_state.reshape(1, head_count * head_width, state_width).astype(jnp.bfloat16),
        SEQ,
        split_axis=1,
        concat_axis=0,
        tiled=True,
    ).astype(jnp.float32)
    decays = gathered_by_axis(span_decay.reshape(1, head_count), SEQ, (0, 1, 2), 0)
    row_head = (own_index * row_share + jnp.arange(row_share, dtype=jnp.int32)) // head_width
    head_pick = (row_head[:, None] == jnp.arange(head_count, dtype=jnp.int32)[None, :]).astype(
        jnp.float32
    )
    block_decay = jnp.dot(
        decays, head_pick.T, precision=lax.Precision.HIGHEST, preferred_element_type=jnp.float32
    )
    block_state = pieces
    lead_decay = jnp.ones_like(block_decay)
    span_range = jnp.arange(span_total, dtype=jnp.int32)
    level_list = []
    for bit_index in range(span_bits):
        other_state = flip_pairs(block_state, bit_index)
        other_decay = flip_pairs(block_decay, bit_index)
        is_upper = span_range >> bit_index & 1 == 1
        level_list.append(
            jnp.where(is_upper[:, None, None], lead_decay[:, :, None] * other_state, 0.0)
        )
        block_state = jnp.where(
            is_upper[:, None, None],
            block_state + block_decay[:, :, None] * other_state,
            other_state + other_decay[:, :, None] * block_state,
        )
        lead_decay = jnp.where(is_upper[:, None], lead_decay * other_decay, lead_decay)
        block_decay = block_decay * other_decay
    level_all = jnp.stack(level_list, 1).astype(jnp.bfloat16)
    returned = lax.all_to_all(level_all, SEQ, split_axis=0, concat_axis=2, tiled=True)
    remote_state = returned.reshape(span_bits, head_count, head_width, state_width)
    level_index = level_of_pairs(tok_rows, STRETCH, low_bits)
    element_position = jnp.arange(tok_rows, dtype=jnp.int32)
    visible = (element_position[:, None] >= element_position[None, :]) & (
        doc_count[:, None] == doc_count[None, :]
    )
    scores = jnp.einsum("tn,sn->ts", query_proj, key_proj, preferred_element_type=jnp.float32)
    reach_decay = jnp.exp(log_total) * (doc_count == 0).astype(jnp.float32)[:, None]
    group_size = math.gcd(head_count, 4)
    group_count = head_count // group_size

    def head_group(inputs):
        group_log, group_weight, group_scaled, group_remote, group_reach = inputs
        select = jnp.zeros((group_size, tok_rows, tok_rows), jnp.float32)
        for level_id in range(low_bits + 1):
            select = select + jnp.where(
                level_index[None] == level_id,
                jnp.transpose(group_weight[:, :, level_id])[:, :, None],
                0.0,
            )
        log_rows = jnp.transpose(group_log)
        log_gap = jnp.where(visible[None], log_rows[:, :, None] - log_rows[:, None, :], -jnp.inf)
        mixing = (scores[None] * select * jnp.exp(log_gap)).astype(jnp.bfloat16)
        local_part = jnp.einsum(
            "hts,shp->thp",
            mixing,
            group_scaled.reshape(tok_rows, group_size, head_width),
            preferred_element_type=jnp.float32,
        )
        projected = jnp.einsum(
            "tn,bhpn->tbhp", query_proj, group_remote, preferred_element_type=jnp.float32
        )
        remote_weight = group_weight[:, :, 1 + low_bits : 1 + low_bits + span_bits]
        remote_part = group_reach[:, :, None] * jnp.einsum(
            "thb,tbhp->thp", remote_weight, projected, precision=lax.Precision.HIGHEST
        )
        return (local_part + remote_part).reshape(tok_rows, group_size * head_width)

    stacked = (
        log_total.reshape(tok_rows, group_count, group_size).transpose(1, 0, 2),
        level_weight.reshape(tok_rows, group_count, group_size, level_count).transpose(1, 0, 2, 3),
        scaled_in.reshape(tok_rows, group_count, group_size * head_width).transpose(1, 0, 2),
        remote_state.reshape(span_bits, group_count, group_size, head_width, state_width).transpose(
            1, 0, 2, 3, 4
        ),
        reach_decay.reshape(tok_rows, group_count, group_size).transpose(1, 0, 2),
    )
    group_parts = lax.map(head_group, stacked)
    both_parts = group_parts.transpose(1, 0, 2).reshape(tok_rows, head_count * head_width)
    combined = both_parts + jnp.repeat(skip_weight, head_width)[None, :] * values_in.astype(
        jnp.float32
    )
    gated_out = combined * jax.nn.silu(gate_in.astype(jnp.float32))
    square_sum = over_copies(jnp.sum(gated_out * gated_out, axis=1), "head")
    mean_square = square_sum / (H * HEADDIM)
    return (gated_out * lax.rsqrt(mean_square + epsilon)[:, None] * norm_gain[None, :]).astype(
        jnp.bfloat16
    )


def solution(mesh):
    split = Mesh(
        mesh.devices.reshape(4, 16, 2, mesh.shape["head"]), ("seq_0", "seq_1", "seq_2", "head")
    )
    placed = (
        P(SEQ, "head"),
        P(SEQ, "head"),
        P(SEQ, None),
        P(SEQ, None),
        P(SEQ, "head"),
        P(SEQ, "head"),
        P("head"),
        P("head"),
        P(None, "head", None),
        P(SEQ),
        P(SEQ),
    )
    return jax.shard_map(
        local, mesh=split, in_specs=placed, out_specs=P(SEQ, "head"), check_vma=False
    )
```

profile of v0, /device:TPU:2, one launch (start us, length us, event | category | flops | bytes accessed | tf_op | source)
XLA Modules:
  0.0 271.4 jit_solution(7450920758946439737)
XLA Ops:
  3.7 1.1 reduce-window.19
  5.1 1.5 copy.349
  7.6 1.4 fusion.30
  10.4 2.2 reduce.9
  13.4 19.5 %all-to-all-start = ((bf16[128,2,512]{2,1,0:T(2,128)(2,1)}), bf16[128,2,512]{2,1,0:T(2,128)(2,1)S(1)}, u32[]{:S(2)}, u32[]{:S(2)}) async-start(bf16[128,2,512]{2,1,0:T(2,128)(2,1)} %reshape.1288), calls=%async_computation | async-start | bytes 524288 | tf_op jit(solution)/shard_map/all_to_all | solution.py:113
  33.1 8.0 %all-gather.3 = f32[4,1,16]{2,1,0:T(1,128)S(1)} all-gather(f32[1,1,16]{2,1,0:T(1,128)S(1)} %bitcast.339), channel_id=2, replica_groups=mesh['seq_0'=4,'seq_1'=16,'seq_2'=2,'head'=4] {'seq_0'}, dimensions={0}, use_global_device_ids=true | all-gather | bytes 320 | tf_op jit(solution)/shard_map/all_gather | solution.py:24
  41.1 29.5 %all-gather.4 = f32[16,4,16]{2,1,0:T(4,128)S(1)} all-gather(f32[1,4,16]{2,1,0:T(4,128)S(1)} %bitcast.338), channel_id=3, replica_groups=mesh['seq_0'=4,'seq_1'=16,'seq_2'=2,'head'=4] {'seq_1'}, dimensions={0}, use_global_device_ids=true | all-gather | bytes 4352 | tf_op jit(solution)/shard_map/all_gather | solution.py:24
  70.7 2.0 all-gather.5
  87.5 1.0 add_select_fusion.4
  88.6 2.5 add_select_fusion.3
  91.0 1.1 rev.45
  92.1 2.8 %add_select_fusion.2 = f32[4,2,16,8,128]{4,3,2,1,0:T(8,128)} fusion(f32[4,2,16,8,128]{4,3,2,1,0:T(8,128)S(1)} %bitcast.269, f32[4,2,16,8,128]{4,3,2,1,0:T(8,128)S(1)} %bitcast.265, f32[4,2,16,8,128]{4,3,2,1,0:T(8,128)S(1)} %bitcast.260, f32[4,2,16,8,128]{4,3,2,1,0:T(8,128)S(1)} %bitcast.247, f32[4,2,16,8,128]{4,3,2,1,0:T(8,128)S(1)} %bitcast.255, ...), kind=kLoop, calls=%fused_computation.60 | loop fusion | flops 2621440 | bytes 3179008 | tf_op jit(solution)/shard_map/jit(_where)/select_n | solution.py:139
  94.9 1.1 rev.47
  96.0 5.8 %add_select_fusion.1 = f32[2,2,32,8,128]{4,3,2,1,0:T(8,128)} fusion(f32[2,2,32,8,128]{4,3,2,1,0:T(8,128)S(1)} %bitcast.274, f32[2,2,32,8,128]{4,3,2,1,0:T(8,128)S(1)} %bitcast.270, f32[2,2,32,8,128]{4,3,2,1,0:T(8,128)S(1)} %bitcast.266, f32[2,2,32,8,128]{4,3,2,1,0:T(8,128)S(1)} %bitcast.261, f32[2,2,32,8,128]{4,3,2,1,0:T(8,128)S(1)} %bitcast.248, ...), kind=kLoop, calls=%fused_computation.58 | loop fusion | flops 3276800 | bytes 3711616 | tf_op jit(solution)/shard_map/jit(_where)/select_n | solution.py:139
  101.8 1.9 rev.49
  103.7 6.6 %add_select_fusion = f32[1,2,64,8,128]{4,3,2,1,0:T(8,128)} fusion(f32[1,2,64,8,128]{4,3,2,1,0:T(8,128)} %bitcast.279, f32[1,2,64,8,128]{4,3,2,1,0:T(8,128)S(1)} %bitcast.275, f32[1,2,64,8,128]{4,3,2,1,0:T(8,128)S(1)} %bitcast.271, f32[1,2,64,8,128]{4,3,2,1,0:T(8,128)S(1)} %bitcast.267, f32[1,2,64,8,128]{4,3,2,1,0:T(8,128)S(1)} %bitcast.262, ...), kind=kLoop, calls=%fused_computation.56 | loop fusion | flops 3932160 | bytes 4244224 | tf_op jit(solution)/shard_map/jit(_where)/select_n | solution.py:139
  110.4 1.9 rev.51
  112.3 0.9 fusion.32
  113.3 2.0 fusion.33
  115.2 1.1 fusion.34
  116.3 1.1 fusion.35
  117.4 1.1 fusion.36
  118.5 1.1 fusion.37
  119.6 1.1 fusion.38
  120.7 14.1 %all-to-all-start.1 = ((bf16[128,7,8,128]{3,2,1,0:T(8,128)(2,1)}), bf16[128,7,8,128]{3,2,1,0:T(8,128)(2,1)S(1)}, u32[]{:S(2)}, u32[]{:S(2)}) async-start(bf16[128,7,8,128]{3,2,1,0:T(8,128)(2,1)} %fusion.38), calls=%async_computation.1 | async-start | bytes 3670016 | tf_op jit(solution)/shard_map/all_to_all | solution.py:147
  136.0 1.3 copy.411
  137.5 1.2 fusion.50
  138.7 84.2 %all-to-all-done.1 = bf16[128,7,8,128]{3,2,1,0:T(8,128)(2,1)S(1)} async-done(((bf16[128,7,8,128]{3,2,1,0:T(8,128)(2,1)}), bf16[128,7,8,128]{3,2,1,0:T(8,128)(2,1)S(1)}, u32[]{:S(2)}, u32[]{:S(2)}) %all-to-all-start.1) | async-done | bytes 1835040 | tf_op jit(solution)/shard_map/all_to_all | solution.py:147
  222.9 1.6 copy.408
  224.5 32.9 %while.12 = (s32[]{:T(128)}, f32[4,512,256]{1,2,0:T(8,128)}, bf16[4,512,256]{1,2,0:T(8,128)(2,1)}, f32[512,512]{1,0:T(8,128)S(1)}, f32[4,512,4,11]{1,2,3,0:T(4,1...) while((s32[]{:T(128)}, f32[4,512,256]{1,2,0:T(8,128)}, ...), condition=%wide.region_4.5_spmd.clone.clone, body=%wide.region_3.4_spmd.clone.clone.sunk | while | flops 387842048 | bytes 8172673 | solution.py:195
  224.5 1.8 fusion.70
  226.4 1.0 constant_dynamic-slice_fusion.2
  227.3 0.9 fusion.69
  228.5 3.4 %fusion.71 = f32[512,4,64]{0,2,1:T(8,128)S(1)} fusion(bf16[512,4,64]{0,2,1:T(8,128)(2,1)S(1)} %bitcast.277, f32[4,512]{1,0:T(4,128)S(1)} %get-tuple-element.349, f32[4,512]{1,0:T(4,128)S(1)} %get-tuple-element.350, f32[4,512]{1,0:T(4,128)S(1)} %get-tuple-element.351, f32[4,512]{1,0:T(4,128)S(1)} %get-tuple-element.352, ...), kind=kOutput, calls=%fused_computation.15.clone.1 | convolution fusion | flops 147062784 | bytes 3719168 | tf_op jit(solution)/shard_map/while/body/eval_jaxpr/hts,shp->thp/dot_general | solution.py:171
  232.8 1.7 fusion.70
  234.6 1.0 constant_dynamic-slice_fusion.2
  235.6 0.9 fusion.69
  236.7 3.4 %fusion.71 = f32[512,4,64]{0,2,1:T(8,128)S(1)} fusion(bf16[512,4,64]{0,2,1:T(8,128)(2,1)S(1)} %bitcast.277, f32[4,512]{1,0:T(4,128)S(1)} %get-tuple-element.349, f32[4,512]{1,0:T(4,128)S(1)} %get-tuple-element.350, f32[4,512]{1,0:T(4,128)S(1)} %get-tuple-element.351, f32[4,512]{1,0:T(4,128)S(1)} %get-tuple-element.352, ...), kind=kOutput, calls=%fused_computation.15.clone.1 | convolution fusion | flops 147062784 | bytes 3719168 | tf_op jit(solution)/shard_map/while/body/eval_jaxpr/hts,shp->thp/dot_general | solution.py:171
  241.0 1.7 fusion.70
  242.8 1.0 constant_dynamic-slice_fusion.2
  244.9 3.4 %fusion.71 = f32[512,4,64]{0,2,1:T(8,128)S(1)} fusion(bf16[512,4,64]{0,2,1:T(8,128)(2,1)S(1)} %bitcast.277, f32[4,512]{1,0:T(4,128)S(1)} %get-tuple-element.349, f32[4,512]{1,0:T(4,128)S(1)} %get-tuple-element.350, f32[4,512]{1,0:T(4,128)S(1)} %get-tuple-element.351, f32[4,512]{1,0:T(4,128)S(1)} %get-tuple-element.352, ...), kind=kOutput, calls=%fused_computation.15.clone.1 | convolution fusion | flops 147062784 | bytes 3719168 | tf_op jit(solution)/shard_map/while/body/eval_jaxpr/hts,shp->thp/dot_general | solution.py:171
  249.2 1.7 fusion.70
  251.0 1.0 constant_dynamic-slice_fusion.2
  252.0 0.9 fusion.69
  253.1 3.4 %fusion.71 = f32[512,4,64]{0,2,1:T(8,128)S(1)} fusion(bf16[512,4,64]{0,2,1:T(8,128)(2,1)S(1)} %bitcast.277, f32[4,512]{1,0:T(4,128)S(1)} %get-tuple-element.349, f32[4,512]{1,0:T(4,128)S(1)} %get-tuple-element.350, f32[4,512]{1,0:T(4,128)S(1)} %get-tuple-element.351, f32[4,512]{1,0:T(4,128)S(1)} %get-tuple-element.352, ...), kind=kOutput, calls=%fused_computation.15.clone.1 | convolution fusion | flops 147062784 | bytes 3719168 | tf_op jit(solution)/shard_map/while/body/eval_jaxpr/hts,shp->thp/dot_general | solution.py:171
  257.4 2.8 %multiply_reduce_fusion = (f32[512]{0:T(512)S(1)}, f32[512,1024]{0,1:T(8,128)S(1)}) fusion(bf16[512,1024]{0,1:T(8,128)(2,1)} %copy.411, bf16[512,1024]{0,1:T(8,128)(2,1)S(1)} %copy-done.2, f32[1024]{0:T(1024)S(1)} %mul.848, f32[4,512,256]{1,2,0:T(8,128)} %get-tuple-element.71), kind=kLoop, calls=%fused_computation.51 | loop fusion | flops 5766656 | bytes 6297600 | tf_op jit(solution)/shard_map/reduce_sum | solution.py:201
  260.2 9.6 %all_to_all.30 = f32[4,1,512]{2,1,0:T(1,128)S(1)} all-to-all(f32[4,1,512]{2,1,0:T(1,128)S(1)} %broadcast_in_dim.337), channel_id=1, replica_groups=mesh['seq_0'=4,'seq_1'=16,'seq_2'=2,'head'=4] {'head'}, dimensions={0} | all-to-all | bytes 16384 | tf_op jit(solution)/shard_map/all_to_all | solution.py:37
  270.1 1.3 copy.413
  (200 shorter events, 28.2 us)
Async XLA Ops:
  0.0 9.0 %copy-start = (bf16[512,128]{1,0:T(8,128)(2,1)S(1)}, bf16[512,128]{1,0:T(8,128)(2,1)}, u32[]{:S(2)}) copy-start(bf16[512,128]{1,0:T(8,128)(2,1)} %param.15) | copy-start | bytes 393220
  0.0 7.6 %copy-start.19 = (f32[512,16]{0,1:T(8,128)S(1)}, f32[512,16]{0,1:T(8,128)}, u32[]{:S(2)}) copy-start(f32[512,16]{0,1:T(8,128)} %param.17) | copy-start | bytes 98308
  5.1 3.9 %copy-start.15 = (f32[512,16]{0,1:T(8,128)}, f32[512,16]{0,1:T(8,128)S(1)}, u32[]{:S(2)}) copy-start(f32[512,16]{0,1:T(8,128)S(1)} %bitcast_bitcast_fusion) | copy-start | bytes 98308
  6.6 2.8 %copy-start.1 = (bf16[512,1024]{0,1:T(8,128)(2,1)}, bf16[512,1024]{0,1:T(8,128)(2,1)S(1)}, u32[]{:S(2)}) copy-start(bf16[512,1024]{0,1:T(8,128)(2,1)S(1)} %copy.349) | copy-start | bytes 3145732
  13.4 72.8 %all-to-all-start = ((bf16[128,2,512]{2,1,0:T(2,128)(2,1)}), bf16[128,2,512]{2,1,0:T(2,128)(2,1)S(1)}, u32[]{:S(2)}, u32[]{:S(2)}) async-start(bf16[128,2,512]{2,1,0:T(2,128)(2,1)} %reshape.1288), calls=%async_computation | async-start | bytes 524288 | tf_op jit(solution)/shard_map/all_to_all | solution.py:113
  33.0 41.8 %copy-start.22 = (pred[128]{0:T(512)(128)(4,1)}, pred[128]{0:T(512)(128)(4,1)S(1)}, u32[]{:S(2)}) copy-start(pred[128]{0:T(512)(128)(4,1)S(1)} %get-tuple-element.252) | copy-start | bytes 388
  33.0 41.8 %copy-start.24 = (pred[128]{0:T(512)(128)(4,1)}, pred[128]{0:T(512)(128)(4,1)S(1)}, u32[]{:S(2)}) copy-start(pred[128]{0:T(512)(128)(4,1)S(1)} %get-tuple-element.253) | copy-start | bytes 388
  33.0 41.8 %copy-start.26 = (pred[128]{0:T(512)(128)(4,1)}, pred[128]{0:T(512)(128)(4,1)S(1)}, u32[]{:S(2)}) copy-start(pred[128]{0:T(512)(128)(4,1)S(1)} %get-tuple-element.254) | copy-start | bytes 388
  33.0 41.8 %copy-start.28 = (pred[128]{0:T(512)(128)(4,1)}, pred[128]{0:T(512)(128)(4,1)S(1)}, u32[]{:S(2)}) copy-start(pred[128]{0:T(512)(128)(4,1)S(1)} %get-tuple-element.255) | copy-start | bytes 388
  33.1 41.8 %copy-start.30 = (pred[128]{0:T(512)(128)(4,1)}, pred[128]{0:T(512)(128)(4,1)S(1)}, u32[]{:S(2)}) copy-start(pred[128]{0:T(512)(128)(4,1)S(1)} %get-tuple-element.256) | copy-start | bytes 388
  33.1 41.8 %copy-start.32 = (pred[128]{0:T(512)(128)(4,1)}, pred[128]{0:T(512)(128)(4,1)S(1)}, u32[]{:S(2)}) copy-start(pred[128]{0:T(512)(128)(4,1)S(1)} %get-tuple-element.257) | copy-start | bytes 388
  73.7 18.4 %copy-start.4 = (f32[128,8]{1,0:T(8,128)}, f32[128,8]{1,0:T(8,128)S(1)}, u32[]{:S(2)}) copy-start(f32[128,8]{1,0:T(8,128)S(1)} %copy.374) | copy-start | bytes 12292
  73.7 18.4 %copy-start.5 = (f32[16,2,4,8]{3,2,1,0:T(4,128)}, f32[16,2,4,8]{3,2,1,0:T(4,128)S(1)}, u32[]{:S(2)}) copy-start(f32[16,2,4,8]{3,2,1,0:T(4,128)S(1)} %rev.44) | copy-start | bytes 12292
  75.0 17.1 %copy-start.7 = (f32[8,2,8,8]{3,2,1,0:T(8,128)}, f32[8,2,8,8]{3,2,1,0:T(8,128)S(1)}, u32[]{:S(2)}) copy-start(f32[8,2,8,8]{3,2,1,0:T(8,128)S(1)} %copy.429) | copy-start | bytes 12292
  75.1 17.1 %copy-start.8 = (f32[128,8]{1,0:T(8,128)}, f32[128,8]{1,0:T(8,128)S(1)}, u32[]{:S(2)}) copy-start(f32[128,8]{1,0:T(8,128)S(1)} %copy.428) | copy-start | bytes 12292
  103.7 8.6 %copy-start.33 = (pred[128]{0:T(512)(128)(4,1)S(1)}, pred[128]{0:T(512)(128)(4,1)}, u32[]{:S(2)}) copy-start(pred[128]{0:T(512)(128)(4,1)} %copy-done.32) | copy-start | bytes 388
  103.7 9.5 %copy-start.31 = (pred[128]{0:T(512)(128)(4,1)S(1)}, pred[128]{0:T(512)(128)(4,1)}, u32[]{:S(2)}) copy-start(pred[128]{0:T(512)(128)(4,1)} %copy-done.30) | copy-start | bytes 388
  110.3 4.9 %copy-start.14 = (f32[128,8]{1,0:T(8,128)S(1)}, f32[128,8]{1,0:T(8,128)}, u32[]{:S(2)}) copy-start(f32[128,8]{1,0:T(8,128)} %copy.366) | copy-start | bytes 12292
  110.3 4.9 %copy-start.29 = (pred[128]{0:T(512)(128)(4,1)S(1)}, pred[128]{0:T(512)(128)(4,1)}, u32[]{:S(2)}) copy-start(pred[128]{0:T(512)(128)(4,1)} %copy-done.28) | copy-start | bytes 388
  110.3 6.0 %copy-start.13 = (f32[128,8]{1,0:T(8,128)S(1)}, f32[128,8]{1,0:T(8,128)}, u32[]{:S(2)}) copy-start(f32[128,8]{1,0:T(8,128)} %copy.376) | copy-start | bytes 12292
  110.3 6.0 %copy-start.27 = (pred[128]{0:T(512)(128)(4,1)S(1)}, pred[128]{0:T(512)(128)(4,1)}, u32[]{:S(2)}) copy-start(pred[128]{0:T(512)(128)(4,1)} %copy-done.26) | copy-start | bytes 388
  110.3 7.1 %copy-start.12 = (f32[128,8]{1,0:T(8,128)S(1)}, f32[128,8]{1,0:T(8,128)}, u32[]{:S(2)}) copy-start(f32[128,8]{1,0:T(8,128)} %copy.384) | copy-start | bytes 12292
  110.4 7.1 %copy-start.25 = (pred[128]{0:T(512)(128)(4,1)S(1)}, pred[128]{0:T(512)(128)(4,1)}, u32[]{:S(2)}) copy-start(pred[128]{0:T(512)(128)(4,1)} %copy-done.24) | copy-start | bytes 388
  112.3 6.2 %copy-start.3 = (f32[2,2,32,8,128]{4,3,2,1,0:T(8,128)S(1)}, f32[2,2,32,8,128]{4,3,2,1,0:T(8,128)}, u32[]{:S(2)}) copy-start(f32[2,2,32,8,128]{4,3,2,1,0:T(8,128)} %rev.49) | copy-start | bytes 1572868
  112.3 6.2 %copy-start.11 = (f32[128,8]{1,0:T(8,128)S(1)}, f32[128,8]{1,0:T(8,128)}, u32[]{:S(2)}) copy-start(f32[128,8]{1,0:T(8,128)} %copy.390) | copy-start | bytes 12292
  112.3 6.2 %copy-start.23 = (pred[128]{0:T(512)(128)(4,1)S(1)}, pred[128]{0:T(512)(128)(4,1)}, u32[]{:S(2)}) copy-start(pred[128]{0:T(512)(128)(4,1)} %copy-done.22) | copy-start | bytes 388
  113.3 6.3 %copy-start.6 = (f32[1,2,64,8,128]{4,3,2,1,0:T(8,128)S(1)}, f32[1,2,64,8,128]{4,3,2,1,0:T(8,128)}, u32[]{:S(2)}) copy-start(f32[1,2,64,8,128]{4,3,2,1,0:T(8,128)} %rev.51) | copy-start | bytes 1572868
  113.3 6.3 %copy-start.10 = (f32[128,8]{1,0:T(8,128)S(1)}, f32[128,8]{1,0:T(8,128)}, u32[]{:S(2)}) copy-start(f32[128,8]{1,0:T(8,128)} %copy.398) | copy-start | bytes 12292
  113.3 6.3 %copy-start.34 = (pred[128]{0:T(512)(128)(4,1)S(1)}, pred[128]{0:T(512)(128)(4,1)}, u32[]{:S(2)}) copy-start(pred[128]{0:T(512)(128)(4,1)} %and_compare_fusion.21) | copy-start | bytes 388
  119.6 15.2 %copy-start.16 = (f32[512,16]{0,1:T(8,128)S(1)}, f32[512,16]{0,1:T(8,128)}, u32[]{:S(2)}) copy-start(f32[512,16]{0,1:T(8,128)} %copy-done.15) | copy-start | bytes 98308
  119.6 15.2 %copy-start.17 = (f32[512,16]{0,1:T(8,128)S(1)}, f32[512,16]{0,1:T(8,128)}, u32[]{:S(2)}) copy-start(f32[512,16]{0,1:T(8,128)} %get-tuple-element.248) | copy-start | bytes 98308
  120.6 14.2 %copy-start.18 = (f32[16,16,11]{1,0,2:T(8,128)S(1)}, f32[16,16,11]{1,0,2:T(8,128)}, u32[]{:S(2)}) copy-start(f32[16,16,11]{1,0,2:T(8,128)} %param.21) | copy-start | bytes 33796
  120.7 14.7 %copy-start.21 = (s32[512]{0:T(512)S(1)}, s32[512]{0:T(512)}, u32[]{:S(2)}) copy-start(s32[512]{0:T(512)} %param.22) | copy-start | bytes 6148
  120.7 15.3 %copy-start.9 = (bf16[512,1024]{1,0:T(8,128)(2,1)S(1)}, bf16[512,1024]{1,0:T(8,128)(2,1)}, u32[]{:S(2)}) copy-start(bf16[512,1024]{1,0:T(8,128)(2,1)} %param.14) | copy-start | bytes 3145732
  120.7 102.3 %all-to-all-start.1 = ((bf16[128,7,8,128]{3,2,1,0:T(8,128)(2,1)}), bf16[128,7,8,128]{3,2,1,0:T(8,128)(2,1)S(1)}, u32[]{:S(2)}, u32[]{:S(2)}) async-start(bf16[128,7,8,128]{3,2,1,0:T(8,128)(2,1)} %fusion.38), calls=%async_computation.1 | async-start | bytes 3670016 | tf_op jit(solution)/shard_map/all_to_all | solution.py:147
  134.8 2.5 copy-start.35
  224.5 32.9 %copy-start.2 = (bf16[512,1024]{0,1:T(8,128)(2,1)S(1)}, bf16[512,1024]{0,1:T(8,128)(2,1)}, u32[]{:S(2)}) copy-start(bf16[512,1024]{0,1:T(8,128)(2,1)} %copy-done.1) | copy-start | bytes 3145732
  257.4 12.4 %copy-start.20 = (f32[1024]{0:T(1024)S(1)}, f32[1024]{0:T(1024)}, u32[]{:S(2)}) copy-start(f32[1024]{0:T(1024)} %param.20) | copy-start | bytes 12292
where the time goes:
time: 273 us; the launch traced here: 271 us
  waiting for transfers between devices  84.2 us (31%)
  blocking collectives  49.1 us (18%)
  other arithmetic  46.5 us (17%)
  starting transfers between devices  33.6 us (12%)
  local copies, waits for them, and re-layouts  33.5 us (12%)
  matrix products  22.9 us (8%)
    all_to_all x1, waiting for transfers between devices, local(): lax.all_to_all(level_all, SEQ, split_axis=0, concat_axis=2, tiled=True)  84.2 us
    all_gather x3, blocking collectives, gather_in_order(): pieces = lax.all_gather(pieces, axes[k], axis=0, tiled=True)  39.5 us
    all_to_all x1, starting transfers between devices, local(): lax.all_to_all(end_state.reshape(1, head_count * head_width, state_width)...  19.5 us
    select_n x6, other arithmetic, local(): jnp.where(is_upper[:, None, None], block_state + block_decay[:, :, None]...  19.1 us
    all_to_all x1, starting transfers between devices, local(): lax.all_to_all(level_all, SEQ, split_axis=0, concat_axis=2, tiled=True)  14.1 us
    dot_general x4, matrix products, head_group(): jnp.einsum('hts,shp->thp', mixing, group_scaled.reshape(tok_rows, group_s...  13.7 us
    all_to_all x1, blocking collectives, copy_for_each(): lax.all_to_all(jnp.broadcast_to(array[None], (size, *array.shape)), axis,...  9.6 us
    unnamed x7, other arithmetic  9.43 us
  transfers between devices with their start and end apart: 2, of which 1 were waited for; matrix products, arithmetic and copies ran while one was open for 6% of the time, Pallas kernels for 0%

commit v1 on v0

--- a/solution.py
+++ b/solution.py
@@ -21,7 +21,9 @@
 def gather_in_order(array, axes, turns):
     pieces = array[None]
     for k in turns:
-        pieces = lax.all_gather(pieces, axes[k], axis=0, tiled=True)
+        pieces = jnp.concatenate(
+            lax.all_to_all(jnp.stack([pieces] * lax.axis_size(axes[k])), axes[k], 0, 0), axis=0
+        )
     current = [lax.axis_size(axes[k]) for k in reversed(turns)]
     pieces = pieces.reshape(*current, *array.shape)
     turned = sorted(range(len(turns)), key=lambda place: turns[len(turns) - 1 - place])

time: 273 us -> 261 us (0.956)
  blocking collectives: 49.1 us -> 13.3 us
  waiting for transfers between devices: 84.2 us -> 103 us
    all_gather x3 -> x0, blocking collectives: 39.5 us -> none  [gather_in_order(): pieces = lax.all_gather(pieces, axes[k], axis=0, tiled=True)]
    all_to_all x0 -> x2, starting transfers between devices: none -> 20 us  [gather_in_order(): lax.all_to_all(jnp.stack([pieces] * lax.axis_size(axes[k])), axes[k], 0, 0)]
    all_to_all x1, starting transfers between devices: 19.5 us -> 8.14 us  [local(): lax.all_to_all(end_state.reshape(1, head_count * head_width, state_width)...]
    all_to_all x1, waiting for transfers between devices: 0.01 us -> 10.9 us  [local(): lax.all_to_all(end_state.reshape(1, head_count * head_width, state_width)...]
    all_to_all x0 -> x2, waiting for transfers between devices: none -> 8.2 us  [gather_in_order(): lax.all_to_all(jnp.stack([pieces] * lax.axis_size(axes[k])), axes[k], 0, 0)]
    all_to_all x1, starting transfers between devices: 14.1 us -> 7.33 us  [local(): lax.all_to_all(level_all, SEQ, split_axis=0, concat_axis=2, tiled=True)]
    all_to_all x0 -> x1, blocking collectives: none -> 3.71 us  [gather_in_order(): lax.all_to_all(jnp.stack([pieces] * lax.axis_size(axes[k])), axes[k], 0, 0)]
    unnamed x7 -> x8, other arithmetic: 9.43 us -> 9.43 us
  transfers between devices with their start and end apart: 2 -> 4, of which waited for: 1 -> 3; matrix products, arithmetic and copies ran while one was open for 6% -> 10% of each run, Pallas kernels for 0% -> 0%
where the time goes in v1:
time: 261 us; the launch traced here: 259 us
  waiting for transfers between devices  103 us (39%)
  other arithmetic  47 us (18%)
  local copies, waits for them, and re-layouts  35.5 us (14%)
  starting transfers between devices  35.5 us (14%)
  matrix products  22.9 us (9%)
  blocking collectives  13.3 us (5%)
    all_to_all x1, waiting for transfers between devices, local(): lax.all_to_all(level_all, SEQ, split_axis=0, concat_axis=2, tiled=True)  84.2 us
    all_to_all x2, starting transfers between devices, gather_in_order(): lax.all_to_all(jnp.stack([pieces] * lax.axis_size(axes[k])), axes[k], 0, 0)  20 us
    select_n x6, other arithmetic, local(): jnp.where(is_upper[:, None, None], block_state + block_decay[:, :, None]...  19.1 us
    dot_general x4, matrix products, head_group(): jnp.einsum('hts,shp->thp', mixing, group_scaled.reshape(tok_rows, group_s...  13.7 us
    all_to_all x1, waiting for transfers between devices, local(): lax.all_to_all(end_state.reshape(1, head_count * head_width, state_width)...  10.9 us
    all_to_all x1, blocking collectives, copy_for_each(): lax.all_to_all(jnp.broadcast_to(array[None], (size, *array.shape)), axis,...  9.58 us
    unnamed x8, other arithmetic  9.43 us
    all_to_all x2, waiting for transfers between devices, gather_in_order(): lax.all_to_all(jnp.stack([pieces] * lax.axis_size(axes[k])), axes[k], 0, 0)  8.2 us
  transfers between devices with their start and end apart: 4, of which 3 were waited for; matrix products, arithmetic and copies ran while one was open for 10% of the time, Pallas kernels for 0%

profile of v1, /device:TPU:2, one launch (start us, length us, event | category | flops | bytes accessed | tf_op | source)
XLA Modules:
  0.0 259.0 jit_solution(9100354014568095125)
XLA Ops:
  2.4 1.1 reduce-window.19
  5.3 9.1 %all-to-all-start.1 = ((f32[4,1,1,16]{3,2,1,0:T(1,128)}), f32[4,1,1,16]{3,2,1,0:T(1,128)S(1)}, u32[]{:S(2)}, u32[]{:S(2)}) async-start(f32[4,1,1,16]{3,2,1,0:T(1,128)} %stack.9), calls=%async_computation.1 | async-start | bytes 4096 | tf_op jit(solution)/shard_map/all_to_all | solution.py:25
  17.4 1.5 copy.352
  19.7 1.4 fusion.30
  22.2 10.9 %all-to-all-start.2 = ((f32[16,4,1,16]{3,1,2,0:T(4,128)}), f32[16,4,1,16]{3,1,2,0:T(4,128)S(1)}, u32[]{:S(2)}, u32[]{:S(2)}) async-start(f32[16,4,1,16]{3,1,2,0:T(4,128)} %stack.10), calls=%async_computation.2 | async-start | bytes 65536 | tf_op jit(solution)/shard_map/all_to_all | solution.py:25
  34.6 2.2 reduce.7
  37.6 8.2 %all-to-all-done.2 = f32[16,4,1,16]{3,1,2,0:T(4,128)S(1)} async-done(((f32[16,4,1,16]{3,1,2,0:T(4,128)}), f32[16,4,1,16]{3,1,2,0:T(4,128)S(1)}, u32[]{:S(2)}, u32[]{:S(2)}) %all-to-all-start.2) | async-done | bytes 4128 | tf_op jit(solution)/shard_map/all_to_all | solution.py:25
  45.9 3.7 %all_to_all.45 = f32[2,1,1024]{2,1,0:T(1,128)S(1)} all-to-all(f32[2,1,1024]{2,1,0:T(1,128)S(1)} %reshape.1269), channel_id=1, replica_groups=mesh['seq_0'=4,'seq_1'=16,'seq_2'=2,'head'=4] {'seq_2'}, dimensions={0} | all-to-all | bytes 16384 | tf_op jit(solution)/shard_map/all_to_all | solution.py:25
  49.6 8.1 %all-to-all-start = ((bf16[128,2,512]{2,1,0:T(2,128)(2,1)}), bf16[128,2,512]{2,1,0:T(2,128)(2,1)S(1)}, u32[]{:S(2)}, u32[]{:S(2)}) async-start(bf16[128,2,512]{2,1,0:T(2,128)(2,1)} %reshape.1267), calls=%async_computation | async-start | bytes 524288 | tf_op jit(solution)/shard_map/all_to_all | solution.py:115
  69.7 10.9 %all-to-all-done = bf16[128,2,512]{2,1,0:T(2,128)(2,1)S(1)} async-done(((bf16[128,2,512]{2,1,0:T(2,128)(2,1)}), bf16[128,2,512]{2,1,0:T(2,128)(2,1)S(1)}, u32[]{:S(2)}, u32[]{:S(2)}) %all-to-all-start) | async-done | bytes 262176 | tf_op jit(solution)/shard_map/all_to_all | solution.py:115
  81.9 1.0 add_select_fusion.4
  82.9 2.5 add_select_fusion.3
  85.4 1.1 rev.45
  86.5 2.8 %add_select_fusion.2 = f32[4,2,16,8,128]{4,3,2,1,0:T(8,128)} fusion(f32[4,2,16,8,128]{4,3,2,1,0:T(8,128)S(1)} %bitcast.271, f32[4,2,16,8,128]{4,3,2,1,0:T(8,128)S(1)} %bitcast.267, f32[4,2,16,8,128]{4,3,2,1,0:T(8,128)S(1)} %bitcast.262, f32[4,2,16,8,128]{4,3,2,1,0:T(8,128)S(1)} %bitcast.249, f32[4,2,16,8,128]{4,3,2,1,0:T(8,128)S(1)} %bitcast.257, ...), kind=kLoop, calls=%fused_computation.60 | loop fusion | flops 2621440 | bytes 3179008 | tf_op jit(solution)/shard_map/jit(_where)/select_n | solution.py:141
  89.3 1.1 rev.47
  90.3 5.8 %add_select_fusion.1 = f32[2,2,32,8,128]{4,3,2,1,0:T(8,128)} fusion(f32[2,2,32,8,128]{4,3,2,1,0:T(8,128)S(1)} %bitcast.276, f32[2,2,32,8,128]{4,3,2,1,0:T(8,128)S(1)} %bitcast.272, f32[2,2,32,8,128]{4,3,2,1,0:T(8,128)S(1)} %bitcast.268, f32[2,2,32,8,128]{4,3,2,1,0:T(8,128)S(1)} %bitcast.263, f32[2,2,32,8,128]{4,3,2,1,0:T(8,128)S(1)} %bitcast.250, ...), kind=kLoop, calls=%fused_computation.58 | loop fusion | flops 3276800 | bytes 3711616 | tf_op jit(solution)/shard_map/jit(_where)/select_n | solution.py:141
  96.2 1.9 rev.49
  98.1 6.6 %add_select_fusion = f32[1,2,64,8,128]{4,3,2,1,0:T(8,128)} fusion(f32[1,2,64,8,128]{4,3,2,1,0:T(8,128)} %bitcast.281, f32[1,2,64,8,128]{4,3,2,1,0:T(8,128)S(1)} %bitcast.277, f32[1,2,64,8,128]{4,3,2,1,0:T(8,128)S(1)} %bitcast.273, f32[1,2,64,8,128]{4,3,2,1,0:T(8,128)S(1)} %bitcast.269, f32[1,2,64,8,128]{4,3,2,1,0:T(8,128)S(1)} %bitcast.264, ...), kind=kLoop, calls=%fused_computation.56 | loop fusion | flops 3932160 | bytes 4244224 | tf_op jit(solution)/shard_map/jit(_where)/select_n | solution.py:141
  104.7 1.9 rev.51
  106.6 1.0 fusion.32
  107.6 2.0 fusion.33
  109.6 1.1 fusion.34
  110.7 1.1 fusion.35
  111.7 1.1 fusion.36
  112.8 1.1 fusion.37
  113.9 1.1 fusion.38
  115.0 7.3 %all-to-all-start.4 = ((bf16[128,7,8,128]{3,2,1,0:T(8,128)(2,1)}), bf16[128,7,8,128]{3,2,1,0:T(8,128)(2,1)S(1)}, u32[]{:S(2)}, u32[]{:S(2)}) async-start(bf16[128,7,8,128]{3,2,1,0:T(8,128)(2,1)} %fusion.38), calls=%async_computation.4 | async-start | bytes 3670016 | tf_op jit(solution)/shard_map/all_to_all | solution.py:149
  123.6 1.3 copy.415
  125.1 1.2 fusion.51
  126.3 84.2 %all-to-all-done.4 = bf16[128,7,8,128]{3,2,1,0:T(8,128)(2,1)S(1)} async-done(((bf16[128,7,8,128]{3,2,1,0:T(8,128)(2,1)}), bf16[128,7,8,128]{3,2,1,0:T(8,128)(2,1)S(1)}, u32[]{:S(2)}, u32[]{:S(2)}) %all-to-all-start.4) | async-done | bytes 1835040 | tf_op jit(solution)/shard_map/all_to_all | solution.py:149
  210.5 1.6 copy.412
  212.1 32.9 %while.12 = (s32[]{:T(128)}, f32[4,512,256]{1,2,0:T(8,128)}, bf16[4,512,256]{1,2,0:T(8,128)(2,1)}, f32[512,512]{1,0:T(8,128)S(1)}, f32[4,512,4,11]{1,2,3,0:T(4,1...) while((s32[]{:T(128)}, f32[4,512,256]{1,2,0:T(8,128)}, ...), condition=%wide.region_4.5_spmd.clone.clone, body=%wide.region_3.4_spmd.clone.clone.sunk | while | flops 387842048 | bytes 8172673 | solution.py:197
  212.1 1.8 fusion.71
  214.0 1.0 constant_dynamic-slice_fusion.2
  214.9 0.9 fusion.70
  216.1 3.4 %fusion.72 = f32[512,4,64]{0,2,1:T(8,128)S(1)} fusion(bf16[512,4,64]{0,2,1:T(8,128)(2,1)S(1)} %bitcast.279, f32[4,512]{1,0:T(4,128)S(1)} %get-tuple-element.347, f32[4,512]{1,0:T(4,128)S(1)} %get-tuple-element.348, f32[4,512]{1,0:T(4,128)S(1)} %get-tuple-element.349, f32[4,512]{1,0:T(4,128)S(1)} %get-tuple-element.350, ...), kind=kOutput, calls=%fused_computation.15.clone.1 | convolution fusion | flops 147062784 | bytes 3719168 | tf_op jit(solution)/shard_map/while/body/eval_jaxpr/hts,shp->thp/dot_general | solution.py:173
  220.4 1.7 fusion.71
  222.1 1.0 constant_dynamic-slice_fusion.2
  224.3 3.4 %fusion.72 = f32[512,4,64]{0,2,1:T(8,128)S(1)} fusion(bf16[512,4,64]{0,2,1:T(8,128)(2,1)S(1)} %bitcast.279, f32[4,512]{1,0:T(4,128)S(1)} %get-tuple-element.347, f32[4,512]{1,0:T(4,128)S(1)} %get-tuple-element.348, f32[4,512]{1,0:T(4,128)S(1)} %get-tuple-element.349, f32[4,512]{1,0:T(4,128)S(1)} %get-tuple-element.350, ...), kind=kOutput, calls=%fused_computation.15.clone.1 | convolution fusion | flops 147062784 | bytes 3719168 | tf_op jit(solution)/shard_map/while/body/eval_jaxpr/hts,shp->thp/dot_general | solution.py:173
  228.6 1.7 fusion.71
  230.3 1.0 constant_dynamic-slice_fusion.2
  232.5 3.4 %fusion.72 = f32[512,4,64]{0,2,1:T(8,128)S(1)} fusion(bf16[512,4,64]{0,2,1:T(8,128)(2,1)S(1)} %bitcast.279, f32[4,512]{1,0:T(4,128)S(1)} %get-tuple-element.347, f32[4,512]{1,0:T(4,128)S(1)} %get-tuple-element.348, f32[4,512]{1,0:T(4,128)S(1)} %get-tuple-element.349, f32[4,512]{1,0:T(4,128)S(1)} %get-tuple-element.350, ...), kind=kOutput, calls=%fused_computation.15.clone.1 | convolution fusion | flops 147062784 | bytes 3719168 | tf_op jit(solution)/shard_map/while/body/eval_jaxpr/hts,shp->thp/dot_general | solution.py:173
  236.8 1.7 fusion.71
  238.6 1.0 constant_dynamic-slice_fusion.2
  240.7 3.4 %fusion.72 = f32[512,4,64]{0,2,1:T(8,128)S(1)} fusion(bf16[512,4,64]{0,2,1:T(8,128)(2,1)S(1)} %bitcast.279, f32[4,512]{1,0:T(4,128)S(1)} %get-tuple-element.347, f32[4,512]{1,0:T(4,128)S(1)} %get-tuple-element.348, f32[4,512]{1,0:T(4,128)S(1)} %get-tuple-element.349, f32[4,512]{1,0:T(4,128)S(1)} %get-tuple-element.350, ...), kind=kOutput, calls=%fused_computation.15.clone.1 | convolution fusion | flops 147062784 | bytes 3719168 | tf_op jit(solution)/shard_map/while/body/eval_jaxpr/hts,shp->thp/dot_general | solution.py:173
  245.0 2.8 %multiply_reduce_fusion = (f32[512]{0:T(512)S(1)}, f32[512,1024]{0,1:T(8,128)S(1)}) fusion(bf16[512,1024]{0,1:T(8,128)(2,1)} %copy.415, bf16[512,1024]{0,1:T(8,128)(2,1)S(1)} %copy-done.2, f32[1024]{0:T(1024)S(1)} %mul.842, f32[4,512,256]{1,2,0:T(8,128)} %get-tuple-element.71), kind=kLoop, calls=%fused_computation.51 | loop fusion | flops 5766656 | bytes 6297600 | tf_op jit(solution)/shard_map/reduce_sum | solution.py:203
  247.8 9.6 %all_to_all.46 = f32[4,1,512]{2,1,0:T(1,128)S(1)} all-to-all(f32[4,1,512]{2,1,0:T(1,128)S(1)} %broadcast_in_dim.337), channel_id=1, replica_groups=mesh['seq_0'=4,'seq_1'=16,'seq_2'=2,'head'=4] {'head'}, dimensions={0} | all-to-all | bytes 16384 | tf_op jit(solution)/shard_map/all_to_all | solution.py:39
  257.6 1.3 copy.417
  (210 shorter events, 32.6 us)
Async XLA Ops:
  0.0 21.1 %copy-start = (bf16[512,128]{1,0:T(8,128)(2,1)S(1)}, bf16[512,128]{1,0:T(8,128)(2,1)}, u32[]{:S(2)}) copy-start(bf16[512,128]{1,0:T(8,128)(2,1)} %param.15) | copy-start | bytes 393220
  0.0 19.7 %copy-start.19 = (f32[512,16]{0,1:T(8,128)S(1)}, f32[512,16]{0,1:T(8,128)}, u32[]{:S(2)}) copy-start(f32[512,16]{0,1:T(8,128)} %param.17) | copy-start | bytes 98308
  3.8 17.2 %copy-start.15 = (f32[512,16]{0,1:T(8,128)}, f32[512,16]{0,1:T(8,128)S(1)}, u32[]{:S(2)}) copy-start(f32[512,16]{0,1:T(8,128)S(1)} %bitcast_bitcast_fusion) | copy-start | bytes 98308
  5.3 16.3 %all-to-all-start.1 = ((f32[4,1,1,16]{3,2,1,0:T(1,128)}), f32[4,1,1,16]{3,2,1,0:T(1,128)S(1)}, u32[]{:S(2)}, u32[]{:S(2)}) async-start(f32[4,1,1,16]{3,2,1,0:T(1,128)} %stack.9), calls=%async_computation.1 | async-start | bytes 4096 | tf_op jit(solution)/shard_map/all_to_all | solution.py:25
  17.4 47.9 %copy-start.22 = (pred[128]{0:T(512)(128)(4,1)}, pred[128]{0:T(512)(128)(4,1)S(1)}, u32[]{:S(2)}) copy-start(pred[128]{0:T(512)(128)(4,1)S(1)} %get-tuple-element.250) | copy-start | bytes 388
  17.4 47.9 %copy-start.24 = (pred[128]{0:T(512)(128)(4,1)}, pred[128]{0:T(512)(128)(4,1)S(1)}, u32[]{:S(2)}) copy-start(pred[128]{0:T(512)(128)(4,1)S(1)} %get-tuple-element.251) | copy-start | bytes 388
  18.9 2.6 %copy-start.1 = (bf16[512,1024]{0,1:T(8,128)(2,1)}, bf16[512,1024]{0,1:T(8,128)(2,1)S(1)}, u32[]{:S(2)}) copy-start(bf16[512,1024]{0,1:T(8,128)(2,1)S(1)} %copy.352) | copy-start | bytes 3145732
  21.6 43.8 %copy-start.26 = (pred[128]{0:T(512)(128)(4,1)}, pred[128]{0:T(512)(128)(4,1)S(1)}, u32[]{:S(2)}) copy-start(pred[128]{0:T(512)(128)(4,1)S(1)} %get-tuple-element.252) | copy-start | bytes 388
  21.6 43.8 %copy-start.28 = (pred[128]{0:T(512)(128)(4,1)}, pred[128]{0:T(512)(128)(4,1)S(1)}, u32[]{:S(2)}) copy-start(pred[128]{0:T(512)(128)(4,1)S(1)} %get-tuple-element.253) | copy-start | bytes 388
  22.2 23.6 %all-to-all-start.2 = ((f32[16,4,1,16]{3,1,2,0:T(4,128)}), f32[16,4,1,16]{3,1,2,0:T(4,128)S(1)}, u32[]{:S(2)}, u32[]{:S(2)}) async-start(f32[16,4,1,16]{3,1,2,0:T(4,128)} %stack.10), calls=%async_computation.2 | async-start | bytes 65536 | tf_op jit(solution)/shard_map/all_to_all | solution.py:25
  49.6 30.9 %all-to-all-start = ((bf16[128,2,512]{2,1,0:T(2,128)(2,1)}), bf16[128,2,512]{2,1,0:T(2,128)(2,1)S(1)}, u32[]{:S(2)}, u32[]{:S(2)}) async-start(bf16[128,2,512]{2,1,0:T(2,128)(2,1)} %reshape.1267), calls=%async_computation | async-start | bytes 524288 | tf_op jit(solution)/shard_map/all_to_all | solution.py:115
  58.2 23.1 %copy-start.30 = (pred[128]{0:T(512)(128)(4,1)}, pred[128]{0:T(512)(128)(4,1)S(1)}, u32[]{:S(2)}) copy-start(pred[128]{0:T(512)(128)(4,1)S(1)} %get-tuple-element.254) | copy-start | bytes 388
  58.2 23.1 %copy-start.32 = (pred[128]{0:T(512)(128)(4,1)}, pred[128]{0:T(512)(128)(4,1)S(1)}, u32[]{:S(2)}) copy-start(pred[128]{0:T(512)(128)(4,1)S(1)} %get-tuple-element.255) | copy-start | bytes 388
  61.2 25.3 %copy-start.4 = (f32[128,8]{1,0:T(8,128)}, f32[128,8]{1,0:T(8,128)S(1)}, u32[]{:S(2)}) copy-start(f32[128,8]{1,0:T(8,128)S(1)} %copy.378) | copy-start | bytes 12292
  61.2 25.3 %copy-start.5 = (f32[16,2,4,8]{3,2,1,0:T(4,128)}, f32[16,2,4,8]{3,2,1,0:T(4,128)S(1)}, u32[]{:S(2)}) copy-start(f32[16,2,4,8]{3,2,1,0:T(4,128)S(1)} %rev.44) | copy-start | bytes 12292
  61.5 25.0 %copy-start.7 = (f32[128,8]{1,0:T(8,128)}, f32[128,8]{1,0:T(8,128)S(1)}, u32[]{:S(2)}) copy-start(f32[128,8]{1,0:T(8,128)S(1)} %copy.432) | copy-start | bytes 12292
  61.8 24.7 %copy-start.8 = (f32[8,2,8,8]{3,2,1,0:T(8,128)}, f32[8,2,8,8]{3,2,1,0:T(8,128)S(1)}, u32[]{:S(2)}) copy-start(f32[8,2,8,8]{3,2,1,0:T(8,128)S(1)} %copy.433) | copy-start | bytes 12292
  98.1 8.6 %copy-start.33 = (pred[128]{0:T(512)(128)(4,1)S(1)}, pred[128]{0:T(512)(128)(4,1)}, u32[]{:S(2)}) copy-start(pred[128]{0:T(512)(128)(4,1)} %copy-done.32) | copy-start | bytes 388
  98.1 9.5 %copy-start.31 = (pred[128]{0:T(512)(128)(4,1)S(1)}, pred[128]{0:T(512)(128)(4,1)}, u32[]{:S(2)}) copy-start(pred[128]{0:T(512)(128)(4,1)} %copy-done.30) | copy-start | bytes 388
  104.6 4.9 %copy-start.14 = (f32[128,8]{1,0:T(8,128)S(1)}, f32[128,8]{1,0:T(8,128)}, u32[]{:S(2)}) copy-start(f32[128,8]{1,0:T(8,128)} %copy.370) | copy-start | bytes 12292
  104.6 4.9 %copy-start.29 = (pred[128]{0:T(512)(128)(4,1)S(1)}, pred[128]{0:T(512)(128)(4,1)}, u32[]{:S(2)}) copy-start(pred[128]{0:T(512)(128)(4,1)} %copy-done.28) | copy-start | bytes 388
  104.7 6.0 %copy-start.13 = (f32[128,8]{1,0:T(8,128)S(1)}, f32[128,8]{1,0:T(8,128)}, u32[]{:S(2)}) copy-start(f32[128,8]{1,0:T(8,128)} %copy.380) | copy-start | bytes 12292
  104.7 6.0 %copy-start.27 = (pred[128]{0:T(512)(128)(4,1)S(1)}, pred[128]{0:T(512)(128)(4,1)}, u32[]{:S(2)}) copy-start(pred[128]{0:T(512)(128)(4,1)} %copy-done.26) | copy-start | bytes 388
  104.7 7.0 %copy-start.12 = (f32[128,8]{1,0:T(8,128)S(1)}, f32[128,8]{1,0:T(8,128)}, u32[]{:S(2)}) copy-start(f32[128,8]{1,0:T(8,128)} %copy.388) | copy-start | bytes 12292
  104.7 7.0 %copy-start.25 = (pred[128]{0:T(512)(128)(4,1)S(1)}, pred[128]{0:T(512)(128)(4,1)}, u32[]{:S(2)}) copy-start(pred[128]{0:T(512)(128)(4,1)} %copy-done.24) | copy-start | bytes 388
  106.6 6.2 %copy-start.3 = (f32[2,2,32,8,128]{4,3,2,1,0:T(8,128)S(1)}, f32[2,2,32,8,128]{4,3,2,1,0:T(8,128)}, u32[]{:S(2)}) copy-start(f32[2,2,32,8,128]{4,3,2,1,0:T(8,128)} %rev.49) | copy-start | bytes 1572868
  106.6 6.2 %copy-start.11 = (f32[128,8]{1,0:T(8,128)S(1)}, f32[128,8]{1,0:T(8,128)}, u32[]{:S(2)}) copy-start(f32[128,8]{1,0:T(8,128)} %copy.394) | copy-start | bytes 12292
  106.6 6.2 %copy-start.23 = (pred[128]{0:T(512)(128)(4,1)S(1)}, pred[128]{0:T(512)(128)(4,1)}, u32[]{:S(2)}) copy-start(pred[128]{0:T(512)(128)(4,1)} %copy-done.22) | copy-start | bytes 388
  107.6 6.3 %copy-start.6 = (f32[1,2,64,8,128]{4,3,2,1,0:T(8,128)S(1)}, f32[1,2,64,8,128]{4,3,2,1,0:T(8,128)}, u32[]{:S(2)}) copy-start(f32[1,2,64,8,128]{4,3,2,1,0:T(8,128)} %rev.51) | copy-start | bytes 1572868
  107.6 6.3 %copy-start.10 = (f32[128,8]{1,0:T(8,128)S(1)}, f32[128,8]{1,0:T(8,128)}, u32[]{:S(2)}) copy-start(f32[128,8]{1,0:T(8,128)} %copy.402) | copy-start | bytes 12292
  107.6 6.3 %copy-start.34 = (pred[128]{0:T(512)(128)(4,1)S(1)}, pred[128]{0:T(512)(128)(4,1)}, u32[]{:S(2)}) copy-start(pred[128]{0:T(512)(128)(4,1)} %and_compare_fusion.21) | copy-start | bytes 388
  113.9 8.4 %copy-start.16 = (f32[512,16]{0,1:T(8,128)S(1)}, f32[512,16]{0,1:T(8,128)}, u32[]{:S(2)}) copy-start(f32[512,16]{0,1:T(8,128)} %copy-done.15) | copy-start | bytes 98308
  113.9 8.5 %copy-start.17 = (f32[512,16]{0,1:T(8,128)S(1)}, f32[512,16]{0,1:T(8,128)}, u32[]{:S(2)}) copy-start(f32[512,16]{0,1:T(8,128)} %get-tuple-element.246) | copy-start | bytes 98308
  115.0 7.4 %copy-start.18 = (f32[16,16,11]{1,0,2:T(8,128)S(1)}, f32[16,16,11]{1,0,2:T(8,128)}, u32[]{:S(2)}) copy-start(f32[16,16,11]{1,0,2:T(8,128)} %param.21) | copy-start | bytes 33796
  115.0 7.9 %copy-start.21 = (s32[512]{0:T(512)S(1)}, s32[512]{0:T(512)}, u32[]{:S(2)}) copy-start(s32[512]{0:T(512)} %param.22) | copy-start | bytes 6148
  115.0 8.6 %copy-start.9 = (bf16[512,1024]{1,0:T(8,128)(2,1)S(1)}, bf16[512,1024]{1,0:T(8,128)(2,1)}, u32[]{:S(2)}) copy-start(bf16[512,1024]{1,0:T(8,128)(2,1)} %param.14) | copy-start | bytes 3145732
  115.0 95.5 %all-to-all-start.4 = ((bf16[128,7,8,128]{3,2,1,0:T(8,128)(2,1)}), bf16[128,7,8,128]{3,2,1,0:T(8,128)(2,1)S(1)}, u32[]{:S(2)}, u32[]{:S(2)}) async-start(bf16[128,7,8,128]{3,2,1,0:T(8,128)(2,1)} %fusion.38), calls=%async_computation.4 | async-start | bytes 3670016 | tf_op jit(solution)/shard_map/all_to_all | solution.py:149
  122.4 2.5 copy-start.35
  212.1 32.9 %copy-start.2 = (bf16[512,1024]{0,1:T(8,128)(2,1)S(1)}, bf16[512,1024]{0,1:T(8,128)(2,1)}, u32[]{:S(2)}) copy-start(bf16[512,1024]{0,1:T(8,128)(2,1)} %copy-done.1) | copy-start | bytes 3145732
  245.0 12.4 %copy-start.20 = (f32[1024]{0:T(1024)S(1)}, f32[1024]{0:T(1024)}, u32[]{:S(2)}) copy-start(f32[1024]{0:T(1024)} %param.20) | copy-start | bytes 12292
